TPU v7x, 32 devices: a whole 2x2x4 slice. The times are simulated.
32 devices in a mesh: genes: 16 (over z, y, core), cols: 2 (over x).
Axes of the slice: x: 2, y: 2, z: 4, core: 2. Of those that a mesh axis runs over, the one named last changes fastest.
Arguments:
- expression: float32 [384, 40960], P(None, ('genes', 'cols')), may hold values from -200 to 200
- resample: int32 [384], replicated, may hold values from 0 to 383
- labels: int32 [40960, 300], P(('genes', 'cols')), may hold values from 0 to 1, as said below
- ref_kim: float32 [40960], P(('genes', 'cols')), may hold values from 0 to 1
Outputs:
- connectivity: float32 [40960, 300], P(('genes', 'cols'))
- preservation: float32 [2, 300], replicated
Inputs may be any that keep to these rules, and one draw needn't show every extreme that they name: `labels`: each row holds exactly one 1; every module has 32 or more genes.
All inputs are finite; a program needn't handle non-finite values.
Results may differ from a plain program's by a relative error of at most 0.0031.
Values may be sent and summed in bfloat16 or wider, within the bound.
A program may use at most 128 MiB of HBM per device.

v0:
```python
import math
import jax
import jax.numpy as jnp
from jax import lax
from jax.sharding import PartitionSpec as P

G = 40960


def standardize(expression, resample):
    boot = jnp.take(expression, resample, axis=0)
    centered = boot - jnp.mean(boot, axis=0, keepdims=True)
    total = jnp.sum(centered * centered, axis=0, keepdims=True)
    return (centered * lax.rsqrt(total + 1e-06)).astype(jnp.bfloat16)


def local_sums(connectivity, labels, ref_kim):
    member = labels.astype(jnp.float32)
    kim = jnp.sum(connectivity * member, axis=1)
    rowsum = jnp.sum(connectivity, axis=1)
    stacked = jnp.stack(
        [kim, kim * kim, ref_kim, ref_kim * ref_kim, kim * ref_kim, rowsum, jnp.ones_like(kim)],
        axis=1,
    )
    return jnp.dot(
        member.T, stacked, precision=lax.Precision.HIGHEST, preferred_element_type=jnp.float32
    )


def preserve(sums, total_genes):
    counts = sums[:, 6]
    mean_x = sums[:, 0] / (counts * counts)
    var_x = jnp.maximum(sums[:, 1] / (counts * counts * counts) - mean_x * mean_x, 0.0001)
    mean_y = sums[:, 2] / counts
    var_y = jnp.maximum(sums[:, 3] / counts - mean_y * mean_y, 0.01)
    cross = sums[:, 4] / (counts * counts) - mean_x * mean_y
    between = (sums[:, 5] - sums[:, 0]) / (counts * (total_genes - counts))
    density = (mean_x - between) * jnp.sqrt(counts / var_x)
    linked = cross * jnp.sqrt(counts / (var_x * var_y))
    return jnp.stack([density, linked], axis=0)


def tile_term(row_block, column_block, column_ids, module_count):
    scores = lax.dot_general(
        row_block, column_block, (((0,), (0,)), ((), ())), preferred_element_type=jnp.float32
    )
    squares = scores * scores
    adjacency = (squares * squares * squares).astype(jnp.bfloat16)
    member_block = (
        column_ids[:, None] == jnp.arange(module_count, dtype=jnp.int32)[None, :]
    ).astype(jnp.bfloat16)
    return jnp.dot(adjacency, member_block, preferred_element_type=jnp.float32)


def add_tiles(carried, row_block, piece, every_ids, shard_width, module_count):
    span_width = piece.shape[1]
    column_step = shard_width * math.gcd(span_width // shard_width, 8)
    steps_total = span_width // column_step

    def one_step(step_index, accumulated):
        columns = lax.dynamic_slice_in_dim(piece, step_index * column_step, column_step, 1)
        column_ids = lax.dynamic_slice_in_dim(every_ids, step_index * column_step, column_step, 0)
        return accumulated + tile_term(row_block, columns, column_ids, module_count)

    return lax.fori_loop(0, steps_total, one_step, carried)


def local(expression, resample, labels, ref_kim):
    scaled = standardize(expression, resample)
    module_count = labels.shape[1]
    shard_width = scaled.shape[1]
    module_ids = jnp.sum(labels * jnp.arange(module_count, dtype=jnp.int32)[None, :], axis=1)
    row_block = lax.all_gather(scaled, "cols", axis=1, tiled=True)
    panel_ids = lax.all_gather(module_ids, "genes", axis=0, tiled=True)
    initial = jnp.zeros((row_block.shape[1], module_count), jnp.float32)
    partial_value = add_tiles(
        initial,
        row_block,
        lax.all_gather(scaled, "genes", axis=1, tiled=True),
        panel_ids,
        shard_width,
        module_count,
    )
    connectivity = lax.psum_scatter(partial_value, "cols", scatter_dimension=0, tiled=True)
    sums = lax.psum(local_sums(connectivity, labels, ref_kim), ("genes", "cols"))
    return (connectivity, preserve(sums, G))


def solution(mesh):
    placed = (P(None, ("genes", "cols")), P(), P(("genes", "cols"), None), P(("genes", "cols")))
    return jax.shard_map(
        local,
        mesh=mesh,
        in_specs=placed,
        out_specs=(P(("genes", "cols"), None), P()),
        check_vma=False,
    )
```

profile of v0, /device:TPU:0, one launch (start us, length us, event | category | flops | bytes accessed | tf_op | source)
XLA Modules:
  0.0 391.7 jit_solution(1327400909456358095)
XLA Ops:
  7.2 0.0 copy-start
  7.2 0.0 all-gather.6.cloned.1.call-start
  7.2 0.8 compare_select_fusion
  8.0 0.7 compare_and_fusion
  8.7 0.0 copy-done
  8.8 2.7 gather_fusion
  11.5 0.0 copy-start.2
  11.5 1.9 select_reduce_fusion
  13.4 0.2 copy-done.2
  13.6 0.3 multiply_reduce_fusion
  14.0 0.0 copy-start.3
  14.0 1.3 multiply_convert_fusion
  15.2 0.0 all-gather.6.cloned.1.call-update
  15.3 0.0 all-gather.4.cloned.1.call-start
  15.3 0.7 all-gather.4.cloned.1.call-update
  16.0 0.0 reduce-scatter.2.cloned.1.call-start
  16.1 0.0 copy-done.3
  16.1 0.2 multiply_reduce_fusion.2
  16.3 23.3 %all-gather = s32[16,1,1280]{2,1,0:T(1,128)S(1)} all-gather(s32[1,1,1280]{2,1,0:T(1,128)S(1)} %reshape.229), channel_id=1, replica_groups=mesh['genes'=16,'cols'=2] {'genes'}, dimensions={0}, use_global_device_ids=true | all-gather | bytes 87040 | tf_op jit(solution)/shard_map/all_gather | solution.py:74
  39.6 10.2 %all-gather.6.cloned.1.call-done = bf16[384,2560]{1,0:T(8,128)(2,1)} async-done(((bf16[384,1280]{1,0:T(8,128)(2,1)}), bf16[384,2560]{1,0:T(8,128)(2,1)}) %all-gather.6.cloned.1.call-update) | async-done | bytes 1966096 | tf_op jit(solution)/shard_map/all_gather | solution.py:73
  49.8 122.7 %all-gather.4.cloned.1.call-done = bf16[384,20480]{1,0:T(8,128)(2,1)} async-done(((bf16[384,1280]{1,0:T(8,128)(2,1)}), bf16[384,20480]{1,0:T(8,128)(2,1)}) %all-gather.4.cloned.1.call-update) | async-done | bytes 15728656 | tf_op jit(solution)/shard_map/all_gather | solution.py:79
  172.5 124.2 %while.14 = (s32[]{:T(128)}, f32[2560,300]{0,1:T(8,128)}, bf16[384,20480]{1,0:T(8,128)(2,1)}, bf16[384,2560]{1,0:T(8,128)(2,1)}, s32[20480]{0:T(1024)S(1)}, /*index=5*/s32[]{:T(128)}, s32[]{:T(128)}, s32[]{:T(128)}, s32[]{:T(128)}) while((s32[]{:T(128)}, f32[2560,300]{0,1:T(8,128)}, bf16[384,20480]{1,0:T(8,128)(2,1)}, ...), condition=%wide.region_4.5_spmd.clone, body=%wide.region_3.4_spmd.clone.sunk | while | flops 35970764800 | bytes 120955040 | solution.py:65
  172.5 37.4 %fusion.clone.9 = bf16[2560,10240]{0,1:T(8,128)(2,1)} fusion(bf16[384,2560]{1,0:T(8,128)(2,1)} %get-tuple-element.184, bf16[384,20480]{1,0:T(8,128)(2,1)} %get-tuple-element.183, s32[]{:T(128)S(6)} %select_n.27), kind=kOutput, calls=%fused_computation.2.clone.clone.clone.clone.clone.2.clone.1 | convolution fusion | flops 20237516800 | bytes 62259204 | tf_op jit(solution)/shard_map/while/body/eval_jaxpr/dot_general | solution.py:44
  209.9 24.2 %fusion.47 = f32[2560,300]{0,1:T(8,128)} fusion(s32[10240]{0:T(1024)S(1)} %dynamic_slice.28, f32[2560,300]{0,1:T(8,128)} %get-tuple-element.173, pred[]{:T(512)S(6)} %compare.3, bf16[2560,10240]{0,1:T(8,128)(2,1)} %fusion.clone.9), kind=kOutput, calls=%fused_computation.7.clone.3 | convolution fusion | flops 15733248000 | bytes 58613760 | tf_op jit(solution)/shard_map/while/body/eval_jaxpr/dot_general | solution.py:52
  234.1 37.4 %fusion.clone.9 = bf16[2560,10240]{0,1:T(8,128)(2,1)} fusion(bf16[384,2560]{1,0:T(8,128)(2,1)} %get-tuple-element.184, bf16[384,20480]{1,0:T(8,128)(2,1)} %get-tuple-element.183, s32[]{:T(128)S(6)} %select_n.27), kind=kOutput, calls=%fused_computation.2.clone.clone.clone.clone.clone.2.clone.1 | convolution fusion | flops 20237516800 | bytes 62259204 | tf_op jit(solution)/shard_map/while/body/eval_jaxpr/dot_general | solution.py:44
  271.6 25.1 %fusion.47 = f32[2560,300]{0,1:T(8,128)} fusion(s32[10240]{0:T(1024)S(1)} %dynamic_slice.28, f32[2560,300]{0,1:T(8,128)} %get-tuple-element.173, pred[]{:T(512)S(6)} %compare.3, bf16[2560,10240]{0,1:T(8,128)(2,1)} %fusion.clone.9), kind=kOutput, calls=%fused_computation.7.clone.3 | convolution fusion | flops 15733248000 | bytes 58613760 | tf_op jit(solution)/shard_map/while/body/eval_jaxpr/dot_general | solution.py:52
  296.7 0.0 copy-start.5
  296.7 0.0 copy-start.4
  296.7 0.0 reduce-scatter.2.cloned.1.call-update
  296.7 0.7 copy-done.5
  297.4 0.0 copy-start.1
  297.4 40.6 %reduce-scatter.2.cloned.1.call-done = f32[1280,300]{0,1:T(8,128)} async-done(((f32[2560,300]{0,1:T(8,128)}), f32[1280,300]{0,1:T(8,128)}) %reduce-scatter.2.cloned.1.call-update) | async-done | bytes 1536016 | tf_op jit(solution)/shard_map/reduce_scatter | solution.py:84
  338.0 0.0 copy-done.4
  338.0 1.6 fusion.26
  339.7 0.6 stack.27
  340.3 0.6 stack.28
  340.9 0.6 stack_broadcast_in_dim.3
  341.5 1.4 stack.29
  342.9 2.1 fusion.12
  345.0 39.5 %psum.7 = f32[300,7]{0,1:T(8,128)S(1)} all-reduce(f32[300,7]{0,1:T(8,128)S(1)} %fusion.12), channel_id=1, replica_groups=mesh['genes'=16,'cols'=2] {'genes','cols'}, use_global_device_ids=true, to_apply=%region_8.9 | all-reduce | flops 2100 | bytes 16800 | tf_op jit(solution)/shard_map/psum | solution.py:85
  384.6 0.6 pad_maximum_fusion
  385.1 0.0 copy-done.1
  (14 shorter events, 0.1 us)
Async XLA Ops:
  7.2 1.6 copy-start
  7.2 42.6 %all-gather.6.cloned.1.call-start = ((), (), s32[]{:S(2)}) async-start(), calls=%async_computation.2 | async-start | bytes 2949120 | tf_op jit(solution)/shard_map/all_gather | solution.py:73
  11.5 2.1 copy-start.2
  14.0 2.1 copy-start.3
  15.3 157.2 %all-gather.4.cloned.1.call-start = ((), (), s32[]{:S(2)}) async-start(), calls=%async_computation.1 | async-start | bytes 16711680 | tf_op jit(solution)/shard_map/all_gather | solution.py:79
  16.0 322.0 %reduce-scatter.2.cloned.1.call-start = ((), (), s32[]{:S(2)}) async-start(), calls=%async_computation.3 | async-start | bytes 4669440 | tf_op jit(solution)/shard_map/reduce_scatter | solution.py:84
  296.7 0.7 copy-start.5
  296.7 41.4 %copy-start.4 = (s32[1280,300]{0,1:T(8,128)S(1)}, s32[1280,300]{0,1:T(8,128)}, u32[]{:S(2)}) copy-start(s32[1280,300]{0,1:T(8,128)} %param.8) | copy-start | bytes 4608004
  297.4 87.8 %copy-start.1 = (f32[384,1280]{1,0:T(8,128)S(1)}, f32[384,1280]{1,0:T(8,128)}, u32[]{:S(2)}) copy-start(f32[384,1280]{1,0:T(8,128)} %param.6) | copy-start | bytes 5898244
Sparse Core Ops, SparseCore 0:
  15.4 34.3 all-gather.5
  52.6 119.7 all-gather.3
  296.8 41.1 reduce-scatter.1
where the time goes:
time: 392 us
  waiting for transfers between devices  174 us (44%)
  matrix products  126 us (32%)
  blocking collectives  62.8 us (16%)
  between operations  13.9 us (4%)
  other arithmetic  7.47 us (2%)
  local copies, waits for them, and re-layouts  6.83 us (2%)
    all_gather x1, waiting for transfers between devices, local(): lax.all_gather(scaled, 'genes', axis=1, tiled=True)  123 us
    dot_general x2, matrix products, tile_term(): lax.dot_general(row_block, column_block, (((0,), (0,)), ((), ())), prefer...  74.9 us
    dot_general x2, matrix products, tile_term(): return jnp.dot(adjacency, member_block, preferred_element_type=jnp.float32)  49.3 us
    reduce_scatter x1, waiting for transfers between devices, local(): lax.psum_scatter(partial_value, 'cols', scatter_dimension=0, tiled=True)  40.6 us
    psum x1, blocking collectives, local(): lax.psum(local_sums(connectivity, labels, ref_kim), ('genes', 'cols'))  39.5 us
    all_gather x1, blocking collectives, local(): panel_ids = lax.all_gather(module_ids, 'genes', axis=0, tiled=True)  23.3 us
    all_gather x1, waiting for transfers between devices, local(): row_block = lax.all_gather(scaled, 'cols', axis=1, tiled=True)  10.2 us
  transfers between devices with their start and end apart: 3, of which 3 were waited for; matrix products, arithmetic and copies ran while one was open for 0% of the time, Pallas kernels for 0%

commit v1 on v0

--- a/solution.py
+++ b/solution.py
@@ -82,7 +82,9 @@
         module_count,
     )
     connectivity = lax.psum_scatter(partial_value, "cols", scatter_dimension=0, tiled=True)
-    sums = lax.psum(local_sums(connectivity, labels, ref_kim), ("genes", "cols"))
+    sums = jnp.sum(
+        lax.all_gather(local_sums(connectivity, labels, ref_kim), ("genes", "cols")), axis=0
+    )
     return (connectivity, preserve(sums, G))
 
 

time: 392 us -> 422 us (1.077)
  blocking collectives: 62.8 us -> 92.2 us
    all_gather x0 -> x1, blocking collectives: none -> 68.9 us  [local(): lax.all_gather(local_sums(connectivity, labels, ref_kim), ('genes', 'cols'))]
    psum x1 -> x0, blocking collectives: 39.5 us -> none  [local(): lax.psum(local_sums(connectivity, labels, ref_kim), ('genes', 'cols'))]
where the time goes in v1:
time: 422 us; the launch traced here: 421 us
  waiting for transfers between devices  174 us (41%)
  matrix products  126 us (30%)
  blocking collectives  92.2 us (22%)
  between operations  13.9 us (3%)
  other arithmetic  7.66 us (2%)
  local copies, waits for them, and re-layouts  6.83 us (2%)
    all_gather x1, waiting for transfers between devices, local(): lax.all_gather(scaled, 'genes', axis=1, tiled=True)  123 us
    dot_general x2, matrix products, tile_term(): lax.dot_general(row_block, column_block, (((0,), (0,)), ((), ())), prefer...  74.9 us
    all_gather x1, blocking collectives, local(): lax.all_gather(local_sums(connectivity, labels, ref_kim), ('genes', 'cols'))  68.9 us
    dot_general x2, matrix products, tile_term(): return jnp.dot(adjacency, member_block, preferred_element_type=jnp.float32)  49.3 us
    reduce_scatter x1, waiting for transfers between devices, local(): lax.psum_scatter(partial_value, 'cols', scatter_dimension=0, tiled=True)  40.7 us
    all_gather x1, blocking collectives, local(): panel_ids = lax.all_gather(module_ids, 'genes', axis=0, tiled=True)  23.3 us
    all_gather x1, waiting for transfers between devices, local(): row_block = lax.all_gather(scaled, 'cols', axis=1, tiled=True)  10.2 us
  transfers between devices with their start and end apart: 3, of which 3 were waited for; matrix products, arithmetic and copies ran while one was open for 0% of the time, Pallas kernels for 0%

profile of v1, /device:TPU:0, one launch (start us, length us, event | category | flops | bytes accessed | tf_op | source)
XLA Modules:
  0.0 421.3 jit_solution(4930236860352579865)
XLA Ops:
  7.2 0.0 copy-start
  7.2 0.0 all-gather.8.cloned.1.call-start
  7.2 0.8 compare_select_fusion
  8.0 0.7 compare_and_fusion
  8.7 0.0 copy-done
  8.8 2.7 gather_fusion
  11.5 0.0 copy-start.2
  11.5 1.9 select_reduce_fusion
  13.4 0.2 copy-done.2
  13.6 0.3 multiply_reduce_fusion
  14.0 0.0 copy-start.3
  14.0 1.3 multiply_convert_fusion
  15.2 0.0 all-gather.8.cloned.1.call-update
  15.3 0.0 all-gather.6.cloned.1.call-start
  15.3 0.7 all-gather.6.cloned.1.call-update
  16.0 0.0 reduce-scatter.2.cloned.1.call-start
  16.1 0.0 copy-done.3
  16.1 0.2 multiply_reduce_fusion.2
  16.3 23.3 %all-gather.1 = s32[16,1,1280]{2,1,0:T(1,128)S(1)} all-gather(s32[1,1,1280]{2,1,0:T(1,128)S(1)} %reshape.230), channel_id=1, replica_groups=mesh['genes'=16,'cols'=2] {'genes'}, dimensions={0}, use_global_device_ids=true | all-gather | bytes 87040 | tf_op jit(solution)/shard_map/all_gather | solution.py:74
  39.6 10.2 %all-gather.8.cloned.1.call-done = bf16[384,2560]{1,0:T(8,128)(2,1)} async-done(((bf16[384,1280]{1,0:T(8,128)(2,1)}), bf16[384,2560]{1,0:T(8,128)(2,1)}) %all-gather.8.cloned.1.call-update) | async-done | bytes 1966096 | tf_op jit(solution)/shard_map/all_gather | solution.py:73
  49.8 122.7 %all-gather.6.cloned.1.call-done = bf16[384,20480]{1,0:T(8,128)(2,1)} async-done(((bf16[384,1280]{1,0:T(8,128)(2,1)}), bf16[384,20480]{1,0:T(8,128)(2,1)}) %all-gather.6.cloned.1.call-update) | async-done | bytes 15728656 | tf_op jit(solution)/shard_map/all_gather | solution.py:79
  172.5 124.2 %while.14 = (s32[]{:T(128)}, f32[2560,300]{0,1:T(8,128)}, bf16[384,20480]{1,0:T(8,128)(2,1)}, bf16[384,2560]{1,0:T(8,128)(2,1)}, s32[20480]{0:T(1024)S(1)}, /*index=5*/s32[]{:T(128)}, s32[]{:T(128)}, s32[]{:T(128)}, s32[]{:T(128)}) while((s32[]{:T(128)}, f32[2560,300]{0,1:T(8,128)}, bf16[384,20480]{1,0:T(8,128)(2,1)}, ...), condition=%wide.region_4.5_spmd.clone, body=%wide.region_3.4_spmd.clone.sunk | while | flops 35970764800 | bytes 120955040 | solution.py:65
  172.5 37.4 %fusion.clone.9 = bf16[2560,10240]{0,1:T(8,128)(2,1)} fusion(bf16[384,2560]{1,0:T(8,128)(2,1)} %get-tuple-element.184, bf16[384,20480]{1,0:T(8,128)(2,1)} %get-tuple-element.183, s32[]{:T(128)S(6)} %select_n.27), kind=kOutput, calls=%fused_computation.2.clone.clone.clone.clone.clone.2.clone.1 | convolution fusion | flops 20237516800 | bytes 62259204 | tf_op jit(solution)/shard_map/while/body/eval_jaxpr/dot_general | solution.py:44
  209.9 24.2 %fusion.47 = f32[2560,300]{0,1:T(8,128)} fusion(s32[10240]{0:T(1024)S(1)} %dynamic_slice.28, f32[2560,300]{0,1:T(8,128)} %get-tuple-element.173, pred[]{:T(512)S(6)} %compare.3, bf16[2560,10240]{0,1:T(8,128)(2,1)} %fusion.clone.9), kind=kOutput, calls=%fused_computation.7.clone.3 | convolution fusion | flops 15733248000 | bytes 58613760 | tf_op jit(solution)/shard_map/while/body/eval_jaxpr/dot_general | solution.py:52
  234.1 37.4 %fusion.clone.9 = bf16[2560,10240]{0,1:T(8,128)(2,1)} fusion(bf16[384,2560]{1,0:T(8,128)(2,1)} %get-tuple-element.184, bf16[384,20480]{1,0:T(8,128)(2,1)} %get-tuple-element.183, s32[]{:T(128)S(6)} %select_n.27), kind=kOutput, calls=%fused_computation.2.clone.clone.clone.clone.clone.2.clone.1 | convolution fusion | flops 20237516800 | bytes 62259204 | tf_op jit(solution)/shard_map/while/body/eval_jaxpr/dot_general | solution.py:44
  271.6 25.1 %fusion.47 = f32[2560,300]{0,1:T(8,128)} fusion(s32[10240]{0:T(1024)S(1)} %dynamic_slice.28, f32[2560,300]{0,1:T(8,128)} %get-tuple-element.173, pred[]{:T(512)S(6)} %compare.3, bf16[2560,10240]{0,1:T(8,128)(2,1)} %fusion.clone.9), kind=kOutput, calls=%fused_computation.7.clone.3 | convolution fusion | flops 15733248000 | bytes 58613760 | tf_op jit(solution)/shard_map/while/body/eval_jaxpr/dot_general | solution.py:52
  296.7 0.0 copy-start.5
  296.7 0.0 copy-start.4
  296.7 0.0 reduce-scatter.2.cloned.1.call-update
  296.7 0.7 copy-done.5
  297.4 40.7 %reduce-scatter.2.cloned.1.call-done = f32[1280,300]{0,1:T(8,128)} async-done(((f32[2560,300]{0,1:T(8,128)}), f32[1280,300]{0,1:T(8,128)}) %reduce-scatter.2.cloned.1.call-update) | async-done | bytes 1536016 | tf_op jit(solution)/shard_map/reduce_scatter | solution.py:84
  338.1 0.0 copy-done.4
  338.1 0.0 copy-start.1
  338.1 1.8 fusion.26
  339.9 0.6 stack.27
  340.5 0.6 stack.28
  341.1 0.6 stack_broadcast_in_dim.3
  341.7 1.4 stack.29
  343.1 2.1 fusion.12
  345.2 68.9 %all-gather.2 = f32[32,300,7]{1,2,0:T(8,128)S(1)} all-gather(f32[1,300,7]{1,2,0:T(8,128)S(1)} %fusion.12), channel_id=2, replica_groups=mesh['genes'=16,'cols'=2] {'genes','cols'}, dimensions={0}, use_global_device_ids=true | all-gather | bytes 277200 | tf_op jit(solution)/shard_map/all_gather | solution.py:86
  414.2 0.6 pad_maximum_fusion
  414.8 0.0 copy-done.1
  (15 shorter events, 0.2 us)
Async XLA Ops:
  7.2 1.6 copy-start
  7.2 42.6 %all-gather.8.cloned.1.call-start = ((), (), s32[]{:S(2)}) async-start(), calls=%async_computation.2 | async-start | bytes 2949120 | tf_op jit(solution)/shard_map/all_gather | solution.py:73
  11.5 2.1 copy-start.2
  14.0 2.1 copy-start.3
  15.3 157.2 %all-gather.6.cloned.1.call-start = ((), (), s32[]{:S(2)}) async-start(), calls=%async_computation.1 | async-start | bytes 16711680 | tf_op jit(solution)/shard_map/all_gather | solution.py:79
  16.0 322.1 %reduce-scatter.2.cloned.1.call-start = ((), (), s32[]{:S(2)}) async-start(), calls=%async_computation.3 | async-start | bytes 4669440 | tf_op jit(solution)/shard_map/reduce_scatter | solution.py:84
  296.7 0.7 copy-start.5
  296.7 41.4 %copy-start.4 = (s32[1280,300]{0,1:T(8,128)S(1)}, s32[1280,300]{0,1:T(8,128)}, u32[]{:S(2)}) copy-start(s32[1280,300]{0,1:T(8,128)} %param.8) | copy-start | bytes 4608004
  338.1 76.7 %copy-start.1 = (f32[384,1280]{1,0:T(8,128)S(1)}, f32[384,1280]{1,0:T(8,128)}, u32[]{:S(2)}) copy-start(f32[384,1280]{1,0:T(8,128)} %param.6) | copy-start | bytes 5898244
Sparse Core Ops, SparseCore 0:
  15.4 34.3 all-gather.7
  52.6 119.7 all-gather.5
  296.8 41.1 reduce-scatter.1
